TPU v7x, 32 devices: a whole 2x2x4 slice. The times are simulated.
32 devices in a mesh: ccd: 16 (over z, y, x), row: 2 (over core).
Axes of the slice: x: 2, y: 2, z: 4, core: 2. Of those that a mesh axis runs over, the one named last changes fastest.
Arguments:
- exposure: float32 [16, 48, 2048], P('ccd', 'row'), may hold values from -6 to 6
- row_shift: int32 [16], P('ccd'), may hold values from 0 to 7
- row_fraction: bfloat16 [16, 48], P('ccd', 'row'), may hold values from 0 to 1
- column_shift: int32 [16], P('ccd'), may hold values from 0 to 127
- column_fraction: bfloat16 [16, 2048], P('ccd'), may hold values from 0 to 1
- piece_width: int32 [16, 16], P('ccd'), may hold values from 1 to 128
- route_tile: int32 [16, 16], P('ccd'), may hold values from 0 to 15, as said below
- route_cell: int32 [16, 16], P('ccd'), may hold values from 0 to 31, as said below
- template: float32 [16, 48, 4096], P('ccd', 'row'), may hold values from -6 to 6
- match_kernel: bfloat16 [16, 41, 41], P('ccd'), may hold values from -0.15625 to 0.15625
- detection_kernel: bfloat16 [16, 15, 15], P('ccd'), may hold values from -0.375 to 0.375
Outputs:
- difference: float32 [16, 48, 4096], P('ccd', 'row')
- significance: float32 [16, 48, 4096], P('ccd', 'row')
- noise_level: float32 [], replicated
Inputs may be any that keep to these rules, and one draw needn't show every extreme that they name: Piece p of CCD c lands on tile route_tile[c, p]. Every tile receives at least one piece and at most 32 pieces in all; a quarter of the tiles receive exactly 32. No CCD puts more than 2 pieces on one tile, and some CCDs put exactly 2. `route_cell`: pieces that land on one tile fill different cells.
All inputs are finite; a program needn't handle non-finite values.
Results may differ from a plain program's by a relative error of at most 0.0044.
Values may be sent and summed in bfloat16 or wider, within the bound.
A program may use at most 128 MiB of HBM per device.

v0:
```python
import jax
import jax.numpy as jnp
from jax import lax
from jax.sharding import PartitionSpec as P

PW = 128
PAIR = 2
HALO = 8
KS = 41
DK = 15
stack_depth = 5


def extended_2(x, sides, width):
    for axis, dim in sides:
        size, length = (lax.axis_size(axis), x.shape[dim])
        up = [(i, (i + 1) % size) for i in range(size - 1)]
        down = [(j, i) for i, j in up]
        last = lax.slice_in_dim(x, length - width, length, axis=dim)
        first = lax.slice_in_dim(x, 0, width, axis=dim)
        before = lax.ppermute(last, axis, up)
        after = lax.ppermute(first, axis, down)
        x = jnp.concatenate([before, x, after], axis=dim)
    return x


def passed_along(block, axis, distance):
    devices = range(lax.axis_size(axis))
    route = [(i - distance, i) for i in devices if i - distance in devices]
    return lax.ppermute(block, axis, route)


def warp_columns(padded, column_offset, fraction):
    length = fraction.shape[-1]
    leftward = lax.dynamic_slice_in_dim(padded, column_offset, length, 1).astype(jnp.float32)
    rightward = lax.dynamic_slice_in_dim(padded, column_offset + 1, length, 1).astype(jnp.float32)
    weight = fraction.astype(jnp.float32)[None, :]
    return (1.0 - weight) * leftward + weight * rightward


def band_matrix(kernel):
    extent = kernel.shape[0]
    spread = jnp.arange(2 * PW, dtype=jnp.int32)[:, None] - jnp.arange(PW, dtype=jnp.int32)[None, :]
    picker = (spread[:, :, None] == jnp.arange(extent, dtype=jnp.int32)[None, None, :]).astype(
        jnp.bfloat16
    )
    return jnp.einsum("yd,kjd->ykj", kernel, picker, preferred_element_type=jnp.float32).astype(
        jnp.bfloat16
    )


def banded_filter(source, kernel, height):
    extent = kernel.shape[0]
    margin = extent // 2
    blocks_wide = source.shape[1] // PW
    widened = jnp.pad(source, ((0, 0), (margin, 2 * PW - margin)))
    blocked = widened.reshape(widened.shape[0], blocks_wide + 2, PW)
    windows = jnp.concatenate([blocked[:, :blocks_wide], blocked[:, 1 : blocks_wide + 1]], axis=2)
    banded = band_matrix(kernel)
    running = jnp.zeros((height, blocks_wide, PW), jnp.float32)
    for offset in range(0, extent, stack_depth):
        finish = min(offset + stack_depth, extent)
        stacked = jnp.stack(
            [windows[depth_row : depth_row + height] for depth_row in range(offset, finish)], axis=2
        )
        running = running + jnp.einsum(
            "rcgk,gkj->rcj", stacked, banded[offset:finish], preferred_element_type=jnp.float32
        )
    return running.reshape(height, blocks_wide * PW)


def match_template(template, match_kernel, height):
    rounded = template[0].astype(jnp.bfloat16)
    haloed = extended_2(rounded, (("row", 0),), KS // 2)
    return banded_filter(haloed, match_kernel[0], height)


def detection_pass(difference, detection_kernel, height):
    rounded = difference.astype(jnp.bfloat16)
    haloed = extended_2(rounded, (("row", 0),), DK // 2)
    return banded_filter(haloed, detection_kernel[0], height)


def noise_totals(square_sum, live_count):
    return lax.psum((square_sum, live_count), ("ccd", "row"))


def deliver_pieces(
    exposure,
    row_shift,
    row_fraction,
    column_shift,
    column_fraction,
    piece_width,
    route_tile,
    route_cell,
    cell_count,
):
    exposure_band = exposure[0]
    height = exposure_band.shape[0]
    columns = exposure_band.shape[1]
    pieces = columns // PW
    capacity = lax.axis_size("ccd") * PAIR
    below_rows = passed_along(exposure_band[:HALO], "row", -1)
    extended = jnp.concatenate([exposure_band, below_rows], axis=0)
    weight = row_fraction[0].astype(jnp.float32)[:, None]
    upper_rows = lax.dynamic_slice_in_dim(extended, row_shift[0], height, 0)
    lower_rows = lax.dynamic_slice_in_dim(extended, row_shift[0] + 1, height, 0)
    warped_rows = ((1.0 - weight) * upper_rows + weight * lower_rows).astype(jnp.bfloat16)
    padded = jnp.pad(warped_rows, ((0, 0), (0, PW)))
    piece_tile = route_tile[0]
    piece_cell = route_cell[0]
    widths = piece_width[0]
    order_index = jnp.arange(pieces, dtype=jnp.int32)
    earlier = (piece_tile[:, None] == piece_tile[None, :]) & (
        order_index[None, :] < order_index[:, None]
    )
    piece_rank = jnp.sum(earlier.astype(jnp.int32), axis=1)
    target = piece_tile * PAIR + piece_rank
    chooser = jnp.arange(capacity, dtype=jnp.int32)[:, None] == target[None, :]
    chooser_half = chooser.astype(jnp.bfloat16)
    sent_cell = jnp.sum(jnp.where(chooser, piece_cell[None, :] + 1, 0), axis=1) - 1
    sent_width = jnp.sum(jnp.where(chooser, widths[None, :], 0), axis=1)
    lane_index = jnp.arange(PW, dtype=jnp.int32)
    warped = warp_columns(padded, column_shift[0], column_fraction[0]).astype(jnp.bfloat16)
    keep_mask = (lane_index[None, :] < widths[:, None]).reshape(columns)
    warped = jnp.where(keep_mask[None, :], warped, jnp.zeros((), jnp.bfloat16))
    outgoing = jnp.einsum(
        "sp,rpj->srj",
        chooser_half,
        warped.reshape(height, pieces, PW),
        preferred_element_type=jnp.float32,
    ).astype(jnp.bfloat16)
    incoming, got_cell, got_width = (
        lax.all_to_all(outgoing, "ccd", split_axis=0, concat_axis=0, tiled=True),
        lax.all_to_all(sent_cell, "ccd", split_axis=0, concat_axis=0, tiled=True),
        lax.all_to_all(sent_width, "ccd", split_axis=0, concat_axis=0, tiled=True),
    )
    placer = jnp.arange(cell_count, dtype=jnp.int32)[:, None] == got_cell[None, :]
    science = jnp.einsum(
        "qs,srj->rqj", placer.astype(jnp.bfloat16), incoming, preferred_element_type=jnp.float32
    ).reshape(height, cell_count * PW)
    cell_width = jnp.sum(jnp.where(placer, got_width[None, :], 0), axis=1).astype(jnp.int32)
    live_mask = (lane_index[None, :] < cell_width[:, None]).reshape(cell_count * PW)
    return (science, live_mask, cell_width)


def on_device(
    exposure,
    row_shift,
    row_fraction,
    column_shift,
    column_fraction,
    piece_width,
    route_tile,
    route_cell,
    template,
    match_kernel,
    detection_kernel,
):
    height = exposure.shape[1]
    cell_count = template.shape[2] // PW
    science, live_mask, cell_width = deliver_pieces(
        exposure,
        row_shift,
        row_fraction,
        column_shift,
        column_fraction,
        piece_width,
        route_tile,
        route_cell,
        cell_count,
    )
    matched = match_template(template, match_kernel, height)
    difference = jnp.where(live_mask[None, :], science - matched, jnp.zeros((), jnp.float32))
    square_sum = jnp.sum(difference * difference)
    live_count = (height * jnp.sum(cell_width)).astype(jnp.float32)
    filtered = detection_pass(difference, detection_kernel, height)
    total_square, total_count = noise_totals(square_sum, live_count)
    noise_level = total_square / total_count
    detect_weights = detection_kernel[0].astype(jnp.float32)
    kernel_norm = jnp.sum(detect_weights * detect_weights)
    significance = filtered / jnp.sqrt(1.0 + noise_level * kernel_norm)
    return (difference[None], significance[None], noise_level)


def solution(mesh):
    return jax.shard_map(
        on_device,
        mesh=mesh,
        in_specs=(
            P("ccd", "row", None),
            P("ccd"),
            P("ccd", "row"),
            P("ccd"),
            P("ccd", None),
            P("ccd", None),
            P("ccd", None),
            P("ccd", None),
            P("ccd", "row", None),
            P("ccd", None, None),
            P("ccd", None, None),
        ),
        out_specs=(P("ccd", "row", None), P("ccd", "row", None), P()),
        check_vma=False,
    )
```

profile of v0, /device:TPU:0, one launch (start us, length us, event | category | flops | bytes accessed | tf_op | source)
XLA Modules:
  0.0 126.3 jit_solution(17106949905012191423)
XLA Ops:
  0.6 1.0 convert_element_type.82
  1.7 0.8 slice_bitcast_fusion.10
  2.5 3.1 %collective-permute-start.1 = (bf16[20,4096]{1,0:T(8,128)(2,1)}, bf16[20,4096]{1,0:T(8,128)(2,1)}, u32[]{:S(2)}, u32[]{:S(2)}) collective-permute-start(bf16[20,4096]{1,0:T(8,128)(2,1)} %get-tuple-element.53), channel_id=1, source_target_pairs={{0,1},{2,3},{4,5},{6,7},{8,9},{10,11},{12,13},{14,15},{16,17},{18,... | collective-permute-start | bytes 491528 | tf_op jit(solution)/shard_map/ppermute | solution.py:21
  5.5 1.3 %collective-permute-start.2 = (bf16[20,4096]{1,0:T(8,128)(2,1)}, bf16[20,4096]{1,0:T(8,128)(2,1)}, u32[]{:S(2)}, u32[]{:S(2)}) collective-permute-start(bf16[20,4096]{1,0:T(8,128)(2,1)} %get-tuple-element.54), channel_id=1, source_target_pairs={{1,0},{3,2},{5,4},{7,6},{9,8},{11,10},{13,12},{15,14},{17,16},{19,... | collective-permute-start | bytes 491528 | tf_op jit(solution)/shard_map/ppermute | solution.py:22
  6.8 1.5 %slice_bitcast_fusion.11 = f32[8,2048]{1,0:T(8,128)} fusion(f32[1,24,2048]{2,1,0:T(8,128)} %param.11), kind=kLoop, calls=%fused_computation.369 | loop fusion | bytes 131072 | tf_op jit(solution)/shard_map/slice | solution.py:104
  8.3 1.3 %collective-permute-start = (f32[8,2048]{1,0:T(8,128)}, f32[8,2048]{1,0:T(8,128)}, u32[]{:S(2)}, u32[]{:S(2)}) collective-permute-start(f32[8,2048]{1,0:T(8,128)} %slice_bitcast_fusion.11), channel_id=1, source_target_pairs={{1,0},{3,2},{5,4},{7,6},{9,8},{11,10},{13,12},{15,14},{17,16},{19,... | collective-permute-start | bytes 196616 | tf_op jit(solution)/shard_map/ppermute | solution.py:30
  9.6 0.9 convert_reduce_fusion
  11.7 1.3 select_reduce_fusion.2
  13.7 7.7 %all-to-all-start = ((s32[16,2,1]{1,2,0:T(1,128)}), s32[16,2,1]{1,2,0:T(1,128)}, u32[]{:S(2)}, u32[]{:S(2)}) async-start(s32[16,2,1]{1,2,0:T(1,128)} %bitcast.4), calls=%async_computation | async-start | bytes 16384 | tf_op jit(solution)/shard_map/all_to_all | solution.py:136
  21.4 1.0 convert_bitcast_fusion.1
  22.5 1.6 %convert_bitcast_fusion = bf16[41,256,128]{2,0,1:T(8,128)(2,1)S(1)} fusion(s32[256,128]{1,0:T(8,128)S(1)} %iota_subtract_fusion, bf16[1,41,41]{2,1,0:T(8,128)(2,1)S(1)} %copy-done), kind=kOutput, calls=%fused_computation.83 | convolution fusion | flops 112852992 | bytes 2821410 | tf_op jit(solution)/shard_map/yd,kjd->ykj/dot_general | solution.py:47
  24.1 2.2 %fusion.231 = (bf16[5,256,128]{2,0,1:T(8,128)(2,1)S(1)}, bf16[5,256,128,1]{2,0,1,3:T(8,128)(2,1)}, bf16[5,256,128,1]{2,0,1,3:T(8,128)(2,1)}, bf16[5,256,128,1]{2...) fusion(bf16[41,256,128]{2,0,1:T(8,128)(2,1)S(1)} %convert_bitca, ...), kind=kLoop, calls=%fused_computation.398 | loop fusion | bytes 5242880 | tf_op jit(solution)/shard_map/slice | solution.py:67
  26.3 0.7 slice.412
  32.7 1.3 %all_to_all.14 = s32[16,2,1]{1,0,2:T(8,128)} reshape(s32[32]{0:T(128)} %get-tuple-element.5) | data formatting | bytes 256 | tf_op jit(solution)/shard_map/all_to_all | solution.py:137
  34.0 1.3 %fusion.232 = (bf16[5,256,128]{2,0,1:T(8,128)(2,1)}, bf16[5,256,128,1]{2,0,1,3:T(8,128)(2,1)}, bf16[5,256,128,1]{2,0,1,3:T(8,128)(2,1)}) fusion(bf16[15,256,128]{2,0,1:T(8,128)(2,1)S(1)} %fusion.4), kind=kLoop, calls=%fused_computation.399 | loop fusion | bytes 1966080 | tf_op jit(solution)/shard_map/slice | solution.py:67
  35.3 6.9 %all-to-all-start.1 = ((s32[16,2,1]{1,2,0:T(1,128)}), s32[16,2,1]{1,2,0:T(1,128)S(1)}, u32[]{:S(2)}, u32[]{:S(2)}) async-start(s32[16,2,1]{1,2,0:T(1,128)} %bitcast.401), calls=%async_computation.1 | async-start | bytes 16384 | tf_op jit(solution)/shard_map/all_to_all | solution.py:137
  42.7 1.4 %reduce.8 = s32[16,2]{1,0:T(8,128)S(1)} reduce(s32[16,2,1]{1,2,0:T(1,128)} %all-to-all-done, s32[]{:T(128)} %broadcast.128), dimensions={2}, to_apply=%all_to_all.13.reduce_sub_computation.3 | reduce | bytes 260 | tf_op jit(solution)/shard_map/all_to_all | solution.py:136
  44.2 5.3 %all-to-all-done.1 = s32[16,2,1]{1,2,0:T(1,128)S(1)} async-done(((s32[16,2,1]{1,2,0:T(1,128)}), s32[16,2,1]{1,2,0:T(1,128)S(1)}, u32[]{:S(2)}, u32[]{:S(2)}) %all-to-all-start.1) | async-done | bytes 160 | tf_op jit(solution)/shard_map/all_to_all | solution.py:137
  51.7 1.1 fusion.210
  52.7 0.8 fusion.215
  53.6 1.0 convolution_convert_fusion
  54.6 0.8 copy.95
  55.4 4.4 %all-to-all-start.2 = ((bf16[32,24,128]{2,1,0:T(8,128)(2,1)}), bf16[32,24,128]{2,1,0:T(8,128)(2,1)}, u32[]{:S(2)}, u32[]{:S(2)}) async-start(bf16[32,24,128]{2,1,0:T(8,128)(2,1)} %copy.95), calls=%async_computation.2 | async-start | bytes 393216 | tf_op jit(solution)/shard_map/all_to_all | solution.py:135
  59.7 1.3 %fusion.23 = bf16[64,4352]{1,0:T(8,128)(2,1)S(1)} fusion(bf16[20,4096]{1,0:T(8,128)(2,1)} %collective-permute-done.2, bf16[24,4096]{1,0:T(8,128)(2,1)S(1)} %convert_bitcast_fusion.1, bf16[20,4096]{1,0:T(8,128)(2,1)} %collective-permute-done.1), kind=kLoop, calls=%fused_computation.153 | loop fusion | flops 3342336 | bytes 1081344 | tf_op jit(solution)/shard_map/concatenate | solution.py:23
  69.6 0.8 fusion.12
  70.8 1.8 %multiply_reduce_fusion = (f32[]{:T(128)}, f32[24,32,128]{2,1,0:T(8,128)S(1)}) fusion(pred[32,128]{1,0:T(8,128)(4,1)S(1)} %get-tuple-element.55, f32[24,32,128]{2,1,0:T(8,128)S(1)} %convolution_add_fusion, s32[32]{0:T(128)S(1)} %eq.80, bf16[32,24,128]{2,1,0:T(8,128)(2,1)} %all-to-all-done.2), kind=kOutput, calls=%fused_computation.333 | convolution fusion | flops 6685695 | bytes 987268 | tf_op jit(solution)/shard_map/qs,srj->rqj/dot_general | solution.py:140
  72.9 2.3 %collective-permute-start.3 = (bf16[7,4096]{1,0:T(8,128)(2,1)S(1)}, bf16[7,4096]{1,0:T(8,128)(2,1)S(1)}, u32[]{:S(2)}, u32[]{:S(2)}) collective-permute-start(bf16[7,4096]{1,0:T(8,128)(2,1)S(1)} %get-tuple-element.51), channel_id=1, source_target_pairs={{0,1},{2,3},{4,5},{6,7},{8,9},{10,11},{12,13},{14,15},{16,17},{18,... | collective-permute-start | bytes 172040 | tf_op jit(solution)/shard_map/ppermute | solution.py:21
  75.3 1.3 %collective-permute-start.4 = (bf16[7,4096]{1,0:T(8,128)(2,1)S(1)}, bf16[7,4096]{1,0:T(8,128)(2,1)S(1)}, u32[]{:S(2)}, u32[]{:S(2)}) collective-permute-start(bf16[7,4096]{1,0:T(8,128)(2,1)S(1)} %get-tuple-element.52), channel_id=1, source_target_pairs={{1,0},{3,2},{5,4},{7,6},{9,8},{11,10},{13,12},{15,14},{17,16},{19,... | collective-permute-start | bytes 172040 | tf_op jit(solution)/shard_map/ppermute | solution.py:22
  76.6 0.8 broadcast_select_fusion
  77.4 40.2 %all-reduce.3 = (f32[]{:T(128)}, f32[]{:T(128)}) all-reduce(f32[]{:T(128)} %get-tuple-element.57, f32[]{:T(128)S(6)} %convert_element_type.89), channel_id=1, replica_groups=mesh['ccd'=16,'row'=2] {'ccd','row'}, use_global_device_ids=true, to_apply=%region_5.6 | all-reduce | flops 2 | bytes 16 | tf_op jit(solution)/shard_map/psum | solution.py:85
  121.1 0.8 copy-done.6
  124.4 0.8 div.22
  (107 shorter events, 21.2 us)
Async XLA Ops:
  0.6 21.8 %copy-start = (bf16[1,41,41]{2,1,0:T(8,128)(2,1)S(1)}, bf16[1,41,41]{2,1,0:T(8,128)(2,1)}, u32[]{:S(2)}) copy-start(bf16[1,41,41]{2,1,0:T(8,128)(2,1)} %param.20) | copy-start | bytes 10090
  2.5 57.3 %collective-permute-start.1 = (bf16[20,4096]{1,0:T(8,128)(2,1)}, bf16[20,4096]{1,0:T(8,128)(2,1)}, u32[]{:S(2)}, u32[]{:S(2)}) collective-permute-start(bf16[20,4096]{1,0:T(8,128)(2,1)} %get-tuple-element.53), channel_id=1, source_target_pairs={{0,1},{2,3},{4,5},{6,7},{8,9},{10,11},{12,13},{14,15},{16,17},{18,... | collective-permute-start | bytes 491528 | tf_op jit(solution)/shard_map/ppermute | solution.py:21
  5.5 54.2 %collective-permute-start.2 = (bf16[20,4096]{1,0:T(8,128)(2,1)}, bf16[20,4096]{1,0:T(8,128)(2,1)}, u32[]{:S(2)}, u32[]{:S(2)}) collective-permute-start(bf16[20,4096]{1,0:T(8,128)(2,1)} %get-tuple-element.54), channel_id=1, source_target_pairs={{1,0},{3,2},{5,4},{7,6},{9,8},{11,10},{13,12},{15,14},{17,16},{19,... | collective-permute-start | bytes 491528 | tf_op jit(solution)/shard_map/ppermute | solution.py:22
  8.3 43.4 %collective-permute-start = (f32[8,2048]{1,0:T(8,128)}, f32[8,2048]{1,0:T(8,128)}, u32[]{:S(2)}, u32[]{:S(2)}) collective-permute-start(f32[8,2048]{1,0:T(8,128)} %slice_bitcast_fusion.11), channel_id=1, source_target_pairs={{1,0},{3,2},{5,4},{7,6},{9,8},{11,10},{13,12},{15,14},{17,16},{19,... | collective-permute-start | bytes 196616 | tf_op jit(solution)/shard_map/ppermute | solution.py:30
  11.2 0.6 copy-start.12
  13.7 21.7 %all-to-all-start = ((s32[16,2,1]{1,2,0:T(1,128)}), s32[16,2,1]{1,2,0:T(1,128)}, u32[]{:S(2)}, u32[]{:S(2)}) async-start(s32[16,2,1]{1,2,0:T(1,128)} %bitcast.4), calls=%async_computation | async-start | bytes 16384 | tf_op jit(solution)/shard_map/all_to_all | solution.py:136
  24.0 3.0 %copy-start.14 = (bf16[1,24]{1,0:T(2,128)(2,1)S(1)}, bf16[1,24]{1,0:T(2,128)(2,1)}, u32[]{:S(2)}) copy-start(bf16[1,24]{1,0:T(2,128)(2,1)} %param.13) | copy-start | bytes 148
  24.1 4.2 %copy-start.13 = (s32[1,16]{1,0:T(1,128)S(1)}, s32[1,16]{1,0:T(1,128)}, u32[]{:S(2)}) copy-start(s32[1,16]{1,0:T(1,128)} %param.16) | copy-start | bytes 196
  24.1 4.8 %copy-start.10 = (bf16[1,2048]{1,0:T(2,128)(2,1)S(1)}, bf16[1,2048]{1,0:T(2,128)(2,1)}, u32[]{:S(2)}) copy-start(bf16[1,2048]{1,0:T(2,128)(2,1)} %param.15) | copy-start | bytes 12292
  24.1 6.0 %copy-start.11 = (bf16[1,15,15]{2,1,0:T(8,128)(2,1)S(1)}, bf16[1,15,15]{2,1,0:T(8,128)(2,1)}, u32[]{:S(2)}) copy-start(bf16[1,15,15]{2,1,0:T(8,128)(2,1)} %param.21) | copy-start | bytes 1354
  30.7 20.9 %copy-start.8 = (f32[1,24,2048]{2,1,0:T(8,128)S(1)}, f32[1,24,2048]{2,1,0:T(8,128)}, u32[]{:S(2)}) copy-start(f32[1,24,2048]{2,1,0:T(8,128)} %param.11) | copy-start | bytes 589828
  35.3 14.2 %all-to-all-start.1 = ((s32[16,2,1]{1,2,0:T(1,128)}), s32[16,2,1]{1,2,0:T(1,128)S(1)}, u32[]{:S(2)}, u32[]{:S(2)}) async-start(s32[16,2,1]{1,2,0:T(1,128)} %bitcast.401), calls=%async_computation.1 | async-start | bytes 16384 | tf_op jit(solution)/shard_map/all_to_all | solution.py:137
  55.4 15.5 %all-to-all-start.2 = ((bf16[32,24,128]{2,1,0:T(8,128)(2,1)}), bf16[32,24,128]{2,1,0:T(8,128)(2,1)}, u32[]{:S(2)}, u32[]{:S(2)}) async-start(bf16[32,24,128]{2,1,0:T(8,128)(2,1)} %copy.95), calls=%async_computation.2 | async-start | bytes 393216 | tf_op jit(solution)/shard_map/all_to_all | solution.py:135
  63.4 1.0 copy-start.4
  63.6 1.5 %copy-start.3 = (bf16[5,256,128,1]{2,0,1,3:T(8,128)(2,1)S(1)}, bf16[5,256,128,1]{2,0,1,3:T(8,128)(2,1)}, u32[]{:S(2)}) copy-start(bf16[5,256,128,1]{2,0,1,3:T(8,128)(2,1)} %get-tuple-element.11) | copy-start | bytes 983044
  65.1 1.0 copy-start.2
  65.8 1.1 copy-start.1
  69.6 0.9 copy-start.9
  72.9 46.7 %collective-permute-start.3 = (bf16[7,4096]{1,0:T(8,128)(2,1)S(1)}, bf16[7,4096]{1,0:T(8,128)(2,1)S(1)}, u32[]{:S(2)}, u32[]{:S(2)}) collective-permute-start(bf16[7,4096]{1,0:T(8,128)(2,1)S(1)} %get-tuple-element.51), channel_id=1, source_target_pairs={{0,1},{2,3},{4,5},{6,7},{8,9},{10,11},{12,13},{14,15},{16,17},{18,... | collective-permute-start | bytes 172040 | tf_op jit(solution)/shard_map/ppermute | solution.py:21
  75.3 44.3 %collective-permute-start.4 = (bf16[7,4096]{1,0:T(8,128)(2,1)S(1)}, bf16[7,4096]{1,0:T(8,128)(2,1)S(1)}, u32[]{:S(2)}, u32[]{:S(2)}) collective-permute-start(bf16[7,4096]{1,0:T(8,128)(2,1)S(1)} %get-tuple-element.52), channel_id=1, source_target_pairs={{1,0},{3,2},{5,4},{7,6},{9,8},{11,10},{13,12},{15,14},{17,16},{19,... | collective-permute-start | bytes 172040 | tf_op jit(solution)/shard_map/ppermute | solution.py:22
  120.9 1.1 copy-start.6
  121.1 1.6 %copy-start.5 = (bf16[5,256,128,1]{2,0,1,3:T(8,128)(2,1)S(1)}, bf16[5,256,128,1]{2,0,1,3:T(8,128)(2,1)}, u32[]{:S(2)}) copy-start(bf16[5,256,128,1]{2,0,1,3:T(8,128)(2,1)} %get-tuple-element.19) | copy-start | bytes 983044
  122.6 1.0 copy-start.7
where the time goes:
time: 127 us; the launch traced here: 126 us
  blocking collectives  40.2 us (32%)
  starting transfers between devices  28.2 us (22%)
  other arithmetic  18.6 us (15%)
  local copies, waits for them, and re-layouts  14.7 us (12%)
  matrix products  12.8 us (10%)
  between operations  6.44 us (5%)
  waiting for transfers between devices  5.34 us (4%)
    psum x1, blocking collectives, noise_totals(): return lax.psum((square_sum, live_count), ('ccd', 'row'))  40.2 us
    dot_general x12, matrix products, banded_filter(): jnp.einsum('rcgk,gkj->rcj', stacked, banded[offset:finish], preferred_ele...  7.79 us
    all_to_all x1, starting transfers between devices, deliver_pieces(): lax.all_to_all(sent_cell, 'ccd', split_axis=0, concat_axis=0, tiled=True)  7.73 us
    all_to_all x1, starting transfers between devices, deliver_pieces(): lax.all_to_all(sent_width, 'ccd', split_axis=0, concat_axis=0, tiled=True)  6.86 us
    ppermute x2, starting transfers between devices, extended_2(): before = lax.ppermute(last, axis, up)  5.4 us
    all_to_all x1, waiting for transfers between devices, deliver_pieces(): lax.all_to_all(sent_width, 'ccd', split_axis=0, concat_axis=0, tiled=True)  5.33 us
    all_to_all x1, starting transfers between devices, deliver_pieces(): lax.all_to_all(outgoing, 'ccd', split_axis=0, concat_axis=0, tiled=True)  4.35 us
    slice x3, local copies, waits for them, and re-layouts, banded_filter(): banded[offset:finish]  4.24 us
  transfers between devices with their start and end apart: 8, of which 1 were waited for; matrix products, arithmetic and copies ran while one was open for 27% of the time, Pallas kernels for 0%

commit v1 on v0

--- a/solution.py
+++ b/solution.py
@@ -82,7 +82,13 @@
 
 
 def noise_totals(square_sum, live_count):
-    return lax.psum((square_sum, live_count), ("ccd", "row"))
+
+    def group_sample(my_data):
+        moved = lax.psum(my_data, "row")
+        item_now = lax.psum(moved, "ccd")
+        return item_now
+
+    return group_sample((square_sum, live_count))
 
 
 def deliver_pieces(

time: 127 us -> 133 us (1.047)
  blocking collectives: 40.2 us -> 46 us
    psum x1 -> x2, blocking collectives: 40.2 us -> 46 us  [the longest x1 42.2 us: group_sample(): item_now = lax.psum(moved, 'ccd')]
  transfers between devices with their start and end apart: 8 -> 8, of which waited for: 1 -> 1; matrix products, arithmetic and copies ran while one was open for 27% -> 25% of each run, Pallas kernels for 0% -> 0%
where the time goes in v1:
time: 133 us; the launch traced here: 132 us
  blocking collectives  46 us (35%)
  starting transfers between devices  28.2 us (21%)
  other arithmetic  18.5 us (14%)
  local copies, waits for them, and re-layouts  14.7 us (11%)
  matrix products  12.7 us (10%)
  between operations  6.43 us (5%)
  waiting for transfers between devices  5.33 us (4%)
    psum x1, blocking collectives, group_sample(): item_now = lax.psum(moved, 'ccd')  42.2 us
    dot_general x12, matrix products, banded_filter(): jnp.einsum('rcgk,gkj->rcj', stacked, banded[offset:finish], preferred_ele...  7.78 us
    all_to_all x1, starting transfers between devices, deliver_pieces(): lax.all_to_all(sent_cell, 'ccd', split_axis=0, concat_axis=0, tiled=True)  7.73 us
    all_to_all x1, starting transfers between devices, deliver_pieces(): lax.all_to_all(sent_width, 'ccd', split_axis=0, concat_axis=0, tiled=True)  6.85 us
    ppermute x2, starting transfers between devices, extended_2(): before = lax.ppermute(last, axis, up)  5.39 us
    all_to_all x1, waiting for transfers between devices, deliver_pieces(): lax.all_to_all(sent_width, 'ccd', split_axis=0, concat_axis=0, tiled=True)  5.32 us
    all_to_all x1, starting transfers between devices, deliver_pieces(): lax.all_to_all(outgoing, 'ccd', split_axis=0, concat_axis=0, tiled=True)  4.35 us
    slice x3, local copies, waits for them, and re-layouts, banded_filter(): banded[offset:finish]  4.23 us
  transfers between devices with their start and end apart: 8, of which 1 were waited for; matrix products, arithmetic and copies ran while one was open for 25% of the time, Pallas kernels for 0%

profile of v1, /device:TPU:0, one launch (start us, length us, event | category | flops | bytes accessed | tf_op | source)
XLA Modules:
  0.0 131.8 jit_solution(885794268401327708)
XLA Ops:
  0.6 1.0 convert_element_type.82
  1.7 0.8 slice_bitcast_fusion.10
  2.5 3.1 %collective-permute-start.1 = (bf16[20,4096]{1,0:T(8,128)(2,1)}, bf16[20,4096]{1,0:T(8,128)(2,1)}, u32[]{:S(2)}, u32[]{:S(2)}) collective-permute-start(bf16[20,4096]{1,0:T(8,128)(2,1)} %get-tuple-element.55), channel_id=1, source_target_pairs={{0,1},{2,3},{4,5},{6,7},{8,9},{10,11},{12,13},{14,15},{16,17},{18,... | collective-permute-start | bytes 491528 | tf_op jit(solution)/shard_map/ppermute | solution.py:21
  5.5 1.3 collective-permute-start.2
  6.8 1.5 %slice_bitcast_fusion.11 = f32[8,2048]{1,0:T(8,128)} fusion(f32[1,24,2048]{2,1,0:T(8,128)} %param.11), kind=kLoop, calls=%fused_computation.369 | loop fusion | bytes 131072 | tf_op jit(solution)/shard_map/slice | solution.py:110
  8.3 1.3 collective-permute-start
  9.6 0.9 convert_reduce_fusion
  11.7 1.3 select_reduce_fusion.2
  13.6 7.7 %all-to-all-start = ((s32[16,2,1]{1,2,0:T(1,128)}), s32[16,2,1]{1,2,0:T(1,128)}, u32[]{:S(2)}, u32[]{:S(2)}) async-start(s32[16,2,1]{1,2,0:T(1,128)} %bitcast.4), calls=%async_computation | async-start | bytes 16384 | tf_op jit(solution)/shard_map/all_to_all | solution.py:142
  21.4 1.0 convert_bitcast_fusion.1
  22.4 1.6 %convert_bitcast_fusion = bf16[41,256,128]{2,0,1:T(8,128)(2,1)S(1)} fusion(s32[256,128]{1,0:T(8,128)S(1)} %iota_subtract_fusion, bf16[1,41,41]{2,1,0:T(8,128)(2,1)S(1)} %copy-done), kind=kOutput, calls=%fused_computation.83 | convolution fusion | flops 112852992 | bytes 2821410 | tf_op jit(solution)/shard_map/yd,kjd->ykj/dot_general | solution.py:47
  24.0 2.2 %fusion.231 = (bf16[5,256,128]{2,0,1:T(8,128)(2,1)S(1)}, bf16[5,256,128,1]{2,0,1,3:T(8,128)(2,1)}, bf16[5,256,128,1]{2,0,1,3:T(8,128)(2,1)}, bf16[5,256,128,1]{2...) fusion(bf16[41,256,128]{2,0,1:T(8,128)(2,1)S(1)} %convert_bitca, ...), kind=kLoop, calls=%fused_computation.398 | loop fusion | bytes 5242880 | tf_op jit(solution)/shard_map/slice | solution.py:67
  32.5 1.3 %all_to_all.14 = s32[16,2,1]{1,0,2:T(8,128)} reshape(s32[32]{0:T(128)} %get-tuple-element.5) | data formatting | bytes 256 | tf_op jit(solution)/shard_map/all_to_all | solution.py:143
  33.9 1.3 fusion.232
  35.2 6.9 %all-to-all-start.1 = ((s32[16,2,1]{1,2,0:T(1,128)}), s32[16,2,1]{1,2,0:T(1,128)S(1)}, u32[]{:S(2)}, u32[]{:S(2)}) async-start(s32[16,2,1]{1,2,0:T(1,128)} %bitcast.401), calls=%async_computation.1 | async-start | bytes 16384 | tf_op jit(solution)/shard_map/all_to_all | solution.py:143
  42.5 1.4 %reduce.8 = s32[16,2]{1,0:T(8,128)S(1)} reduce(s32[16,2,1]{1,2,0:T(1,128)} %all-to-all-done, s32[]{:T(128)} %broadcast.128), dimensions={2}, to_apply=%all_to_all.13.reduce_sub_computation.3 | reduce | bytes 260 | tf_op jit(solution)/shard_map/all_to_all | solution.py:142
  44.0 5.3 %all-to-all-done.1 = s32[16,2,1]{1,2,0:T(1,128)S(1)} async-done(((s32[16,2,1]{1,2,0:T(1,128)}), s32[16,2,1]{1,2,0:T(1,128)S(1)}, u32[]{:S(2)}, u32[]{:S(2)}) %all-to-all-start.1) | async-done | bytes 160 | tf_op jit(solution)/shard_map/all_to_all | solution.py:143
  51.5 1.1 fusion.210
  52.5 0.8 fusion.215
  53.4 0.9 convolution_convert_fusion
  54.3 0.8 copy.95
  55.1 4.4 %all-to-all-start.2 = ((bf16[32,24,128]{2,1,0:T(8,128)(2,1)}), bf16[32,24,128]{2,1,0:T(8,128)(2,1)}, u32[]{:S(2)}, u32[]{:S(2)}) async-start(bf16[32,24,128]{2,1,0:T(8,128)(2,1)} %copy.95), calls=%async_computation.2 | async-start | bytes 393216 | tf_op jit(solution)/shard_map/all_to_all | solution.py:141
  59.5 1.3 fusion.23
  69.4 0.8 fusion.12
  70.6 1.8 %multiply_reduce_fusion = (f32[]{:T(128)}, f32[24,32,128]{2,1,0:T(8,128)S(1)}) fusion(pred[32,128]{1,0:T(8,128)(4,1)S(1)} %get-tuple-element.57, f32[24,32,128]{2,1,0:T(8,128)S(1)} %convolution_add_fusion, s32[32]{0:T(128)S(1)} %eq.80, bf16[32,24,128]{2,1,0:T(8,128)(2,1)} %all-to-all-done.2), kind=kOutput, calls=%fused_computation.333 | convolution fusion | flops 6685695 | bytes 987268 | tf_op jit(solution)/shard_map/qs,srj->rqj/dot_general | solution.py:146
  72.7 2.3 %collective-permute-start.3 = (bf16[7,4096]{1,0:T(8,128)(2,1)S(1)}, bf16[7,4096]{1,0:T(8,128)(2,1)S(1)}, u32[]{:S(2)}, u32[]{:S(2)}) collective-permute-start(bf16[7,4096]{1,0:T(8,128)(2,1)S(1)} %get-tuple-element.53), channel_id=1, source_target_pairs={{0,1},{2,3},{4,5},{6,7},{8,9},{10,11},{12,13},{14,15},{16,17},{18,... | collective-permute-start | bytes 172040 | tf_op jit(solution)/shard_map/ppermute | solution.py:21
  75.0 1.3 collective-permute-start.4
  76.3 0.8 broadcast_select_fusion
  77.1 3.9 %all-reduce.4 = (f32[]{:T(128)}, f32[]{:T(128)}) all-reduce(f32[]{:T(128)} %get-tuple-element.59, f32[]{:T(128)S(6)} %convert_element_type.89), channel_id=1, replica_groups=mesh['ccd'=16,'row'=2] {'row'}, use_global_device_ids=true, to_apply=%region_5.6 | all-reduce | flops 2 | bytes 16 | tf_op jit(solution)/shard_map/psum | solution.py:87
  81.0 42.2 %all-reduce.3 = (f32[]{:T(128)}, f32[]{:T(128)}) all-reduce(f32[]{:T(128)} %get-tuple-element.9, f32[]{:T(128)} %get-tuple-element.10), channel_id=1, replica_groups=mesh['ccd'=16,'row'=2] {'ccd'}, use_global_device_ids=true, to_apply=%region_6.7 | all-reduce | flops 2 | bytes 16 | tf_op jit(solution)/shard_map/psum | solution.py:88
  126.7 0.8 copy-done.6
  129.9 0.8 div.22
  (108 shorter events, 21.8 us)
Async XLA Ops:
  0.6 21.8 %copy-start = (bf16[1,41,41]{2,1,0:T(8,128)(2,1)S(1)}, bf16[1,41,41]{2,1,0:T(8,128)(2,1)}, u32[]{:S(2)}) copy-start(bf16[1,41,41]{2,1,0:T(8,128)(2,1)} %param.20) | copy-start | bytes 10090
  2.5 57.0 %collective-permute-start.1 = (bf16[20,4096]{1,0:T(8,128)(2,1)}, bf16[20,4096]{1,0:T(8,128)(2,1)}, u32[]{:S(2)}, u32[]{:S(2)}) collective-permute-start(bf16[20,4096]{1,0:T(8,128)(2,1)} %get-tuple-element.55), channel_id=1, source_target_pairs={{0,1},{2,3},{4,5},{6,7},{8,9},{10,11},{12,13},{14,15},{16,17},{18,... | collective-permute-start | bytes 491528 | tf_op jit(solution)/shard_map/ppermute | solution.py:21
  5.5 54.0 %collective-permute-start.2 = (bf16[20,4096]{1,0:T(8,128)(2,1)}, bf16[20,4096]{1,0:T(8,128)(2,1)}, u32[]{:S(2)}, u32[]{:S(2)}) collective-permute-start(bf16[20,4096]{1,0:T(8,128)(2,1)} %get-tuple-element.56), channel_id=1, source_target_pairs={{1,0},{3,2},{5,4},{7,6},{9,8},{11,10},{13,12},{15,14},{17,16},{19,... | collective-permute-start | bytes 491528 | tf_op jit(solution)/shard_map/ppermute | solution.py:22
  8.3 43.2 %collective-permute-start = (f32[8,2048]{1,0:T(8,128)}, f32[8,2048]{1,0:T(8,128)}, u32[]{:S(2)}, u32[]{:S(2)}) collective-permute-start(f32[8,2048]{1,0:T(8,128)} %slice_bitcast_fusion.11), channel_id=1, source_target_pairs={{1,0},{3,2},{5,4},{7,6},{9,8},{11,10},{13,12},{15,14},{17,16},{19,... | collective-permute-start | bytes 196616 | tf_op jit(solution)/shard_map/ppermute | solution.py:30
  11.2 0.5 copy-start.12
  13.6 21.5 %all-to-all-start = ((s32[16,2,1]{1,2,0:T(1,128)}), s32[16,2,1]{1,2,0:T(1,128)}, u32[]{:S(2)}, u32[]{:S(2)}) async-start(s32[16,2,1]{1,2,0:T(1,128)} %bitcast.4), calls=%async_computation | async-start | bytes 16384 | tf_op jit(solution)/shard_map/all_to_all | solution.py:142
  24.0 3.0 %copy-start.14 = (bf16[1,24]{1,0:T(2,128)(2,1)S(1)}, bf16[1,24]{1,0:T(2,128)(2,1)}, u32[]{:S(2)}) copy-start(bf16[1,24]{1,0:T(2,128)(2,1)} %param.13) | copy-start | bytes 148
  24.0 4.1 %copy-start.13 = (s32[1,16]{1,0:T(1,128)S(1)}, s32[1,16]{1,0:T(1,128)}, u32[]{:S(2)}) copy-start(s32[1,16]{1,0:T(1,128)} %param.16) | copy-start | bytes 196
  24.0 4.7 %copy-start.10 = (bf16[1,2048]{1,0:T(2,128)(2,1)S(1)}, bf16[1,2048]{1,0:T(2,128)(2,1)}, u32[]{:S(2)}) copy-start(bf16[1,2048]{1,0:T(2,128)(2,1)} %param.15) | copy-start | bytes 12292
  24.0 5.9 %copy-start.11 = (bf16[1,15,15]{2,1,0:T(8,128)(2,1)S(1)}, bf16[1,15,15]{2,1,0:T(8,128)(2,1)}, u32[]{:S(2)}) copy-start(bf16[1,15,15]{2,1,0:T(8,128)(2,1)} %param.21) | copy-start | bytes 1354
  30.6 20.9 %copy-start.8 = (f32[1,24,2048]{2,1,0:T(8,128)S(1)}, f32[1,24,2048]{2,1,0:T(8,128)}, u32[]{:S(2)}) copy-start(f32[1,24,2048]{2,1,0:T(8,128)} %param.11) | copy-start | bytes 589828
  35.2 14.2 %all-to-all-start.1 = ((s32[16,2,1]{1,2,0:T(1,128)}), s32[16,2,1]{1,2,0:T(1,128)S(1)}, u32[]{:S(2)}, u32[]{:S(2)}) async-start(s32[16,2,1]{1,2,0:T(1,128)} %bitcast.401), calls=%async_computation.1 | async-start | bytes 16384 | tf_op jit(solution)/shard_map/all_to_all | solution.py:143
  55.1 15.5 %all-to-all-start.2 = ((bf16[32,24,128]{2,1,0:T(8,128)(2,1)}), bf16[32,24,128]{2,1,0:T(8,128)(2,1)}, u32[]{:S(2)}, u32[]{:S(2)}) async-start(bf16[32,24,128]{2,1,0:T(8,128)(2,1)} %copy.95), calls=%async_computation.2 | async-start | bytes 393216 | tf_op jit(solution)/shard_map/all_to_all | solution.py:141
  63.2 1.0 copy-start.4
  63.4 1.5 %copy-start.3 = (bf16[5,256,128,1]{2,0,1,3:T(8,128)(2,1)S(1)}, bf16[5,256,128,1]{2,0,1,3:T(8,128)(2,1)}, u32[]{:S(2)}) copy-start(bf16[5,256,128,1]{2,0,1,3:T(8,128)(2,1)} %get-tuple-element.13) | copy-start | bytes 983044
  64.9 1.0 copy-start.2
  65.6 1.1 copy-start.1
  69.4 0.9 copy-start.9
  72.7 52.5 %collective-permute-start.3 = (bf16[7,4096]{1,0:T(8,128)(2,1)S(1)}, bf16[7,4096]{1,0:T(8,128)(2,1)S(1)}, u32[]{:S(2)}, u32[]{:S(2)}) collective-permute-start(bf16[7,4096]{1,0:T(8,128)(2,1)S(1)} %get-tuple-element.53), channel_id=1, source_target_pairs={{0,1},{2,3},{4,5},{6,7},{8,9},{10,11},{12,13},{14,15},{16,17},{18,... | collective-permute-start | bytes 172040 | tf_op jit(solution)/shard_map/ppermute | solution.py:21
  75.0 50.1 %collective-permute-start.4 = (bf16[7,4096]{1,0:T(8,128)(2,1)S(1)}, bf16[7,4096]{1,0:T(8,128)(2,1)S(1)}, u32[]{:S(2)}, u32[]{:S(2)}) collective-permute-start(bf16[7,4096]{1,0:T(8,128)(2,1)S(1)} %get-tuple-element.54), channel_id=1, source_target_pairs={{1,0},{3,2},{5,4},{7,6},{9,8},{11,10},{13,12},{15,14},{17,16},{19,... | collective-permute-start | bytes 172040 | tf_op jit(solution)/shard_map/ppermute | solution.py:22
  126.4 1.1 copy-start.6
  126.6 1.6 %copy-start.5 = (bf16[5,256,128,1]{2,0,1,3:T(8,128)(2,1)S(1)}, bf16[5,256,128,1]{2,0,1,3:T(8,128)(2,1)}, u32[]{:S(2)}) copy-start(bf16[5,256,128,1]{2,0,1,3:T(8,128)(2,1)} %get-tuple-element.21) | copy-start | bytes 983044
  128.2 1.0 copy-start.7
